TPU v7x, 256 devices: a whole 4x4x8 slice. The times are simulated.
256 devices in a mesh: row: 8 (over x, z_hi), col: 32 (over y, z_lo, core).
Axes of the slice: x: 4, y: 4, z: 8 (z_hi: 2, z_lo: 4; z = z_hi * 4 + z_lo), core: 2. Of those that a mesh axis runs over, the one named last changes fastest.
Arguments:
- chol_window: bfloat16 [512, 8, 1024], P('row', None, 'col'), may hold values from -6 to 6
- pair_vectors: bfloat16 [512, 512, 1024], P('row', 'col'), may hold values from -0.1875 to 0.1875
- amplitudes: bfloat16 [512, 512, 256], P('row', 'col'), may hold values from -0.0234375 to 0.0234375
Outputs:
- ladder: float32 [8, 256, 512], P(None, 'col', 'row')
All inputs are finite; a program needn't handle non-finite values.
Results may differ from a plain program's by a relative error of at most 0.0029.
Values may be sent and summed in bfloat16 or wider, within the bound.
No kernel may reach another device: no remote copies, remote signals or barrier semaphores. Data moves between devices by JAX's collectives and lax.ppermute only.
A program may use at most 128 MiB of HBM per device.

v0:
```python
import jax
import jax.numpy as jnp
from jax import lax
from jax.sharding import PartitionSpec as P


def from_everyone(x, axis):
    length = lax.axis_size(axis)
    return lax.all_to_all(jnp.broadcast_to(x[None], (length, *x.shape)), axis, 0, 0, tiled=True)


def joined_along(tiles, dim):
    tiles = jnp.moveaxis(tiles, 0, dim)
    dims = tiles.shape
    return tiles.reshape(*dims[:dim], dims[dim] * dims[dim + 1], *dims[dim + 2 :])


def collect(x, axis, dim):
    tiles = from_everyone(x, axis)
    return joined_along(tiles, dim)


def cut_along(x, dim, length):
    before, after = (x.shape[:dim], x.shape[dim + 1 :])
    return jnp.moveaxis(x.reshape(*before, length, -1, *after), dim, 0)


def sent_and_summed(x, axis, dim):
    length = lax.axis_size(axis)
    tiles = lax.all_to_all(cut_along(x, dim, length), axis, 0, 0, tiled=True)
    return jnp.sum(tiles, axis=0)


def local(chol_window, pair_vectors, amplitudes):
    window = collect(chol_window, "col", 2)
    c_rows, width_a, chol_count = window.shape
    block_rows = pair_vectors.shape[0]
    d_cols = pair_vectors.shape[1]
    pair_count = amplitudes.shape[2]

    def ladder_term(chol_rows, vectors_flat, amplitude_block, b_rows):
        integrals = lax.dot_general(
            chol_rows.reshape(-1, chol_count),
            vectors_flat,
            (((1,), (1,)), ((), ())),
            preferred_element_type=jnp.float32,
        )
        integrals = integrals.astype(jnp.bfloat16).reshape(
            chol_rows.shape[0], width_a, b_rows, d_cols
        )
        return jnp.einsum(
            "cabd,cdn->anb", integrals, amplitude_block, preferred_element_type=jnp.float32
        )

    vectors_flat = pair_vectors.reshape(block_rows * d_cols, chol_count)
    zeros_init = jnp.zeros((width_a, pair_count, block_rows), jnp.float32)
    running = zeros_init
    segments = (
        lax.all_gather(window, "row", axis=0, tiled=True),
        lax.all_gather(amplitudes, "row", axis=0, tiled=True),
    )
    row_count = segments[0].shape[0]
    chol_blocks = segments[0].reshape(row_count // c_rows, c_rows, width_a, chol_count)
    amp_blocks = segments[1].reshape(row_count // c_rows, c_rows, d_cols, pair_count)

    def scan_step(carry, operands):
        return (carry + ladder_term(operands[0], vectors_flat, operands[1], block_rows), None)

    running, unused = lax.scan(scan_step, running, (chol_blocks, amp_blocks))
    result = sent_and_summed(running, "col", 1)
    return result


def solution(mesh):
    return jax.shard_map(
        local,
        mesh=mesh,
        in_specs=(P("row", None, "col"), P("row", "col", None), P("row", "col", None)),
        out_specs=P(None, "col", "row"),
        check_vma=False,
    )
```

profile of v0, /device:TPU:1, one launch (start us, length us, event | category | flops | bytes accessed | tf_op | source)
XLA Modules:
  0.0 536.3 jit_solution(9281493108963443618)
XLA Ops:
  9.3 49.2 %all_to_all.10 = bf16[32,2,8192]{2,1,0:T(2,128)(2,1)} all-to-all(bf16[32,2,8192]{2,1,0:T(2,128)(2,1)S(1)} %reshape.32), channel_id=1, replica_groups=mesh['row'=8,'col'=32] {'col'}, dimensions={0} | all-to-all | bytes 2097152 | tf_op jit(solution)/shard_map/all_to_all | solution.py:9
  58.5 3.8 reshape.33
  65.5 60.1 %all-gather.3.cloned.1.call-done = bf16[512,16,256]{2,1,0:T(8,128)(2,1)} async-done(((bf16[64,16,256]{2,1,0:T(8,128)(2,1)}), bf16[512,16,256]{2,1,0:T(8,128)(2,1)}) %all-gather.3.cloned.1.call-update) | async-done | bytes 4194320 | tf_op jit(solution)/shard_map/all_gather | solution.py:60
  125.6 170.1 %all-gather.5.cloned.1.call-done = bf16[512,8,1024]{2,1,0:T(8,128)(2,1)} async-done(((bf16[64,8,1024]{2,1,0:T(8,128)(2,1)}), bf16[512,8,1024]{2,1,0:T(8,128)(2,1)}) %all-gather.5.cloned.1.call-update) | async-done | bytes 8388624 | tf_op jit(solution)/shard_map/all_gather | solution.py:59
  295.7 206.7 %while.11 = (s32[]{:T(128)}, f32[8,256,64]{1,2,0:T(8,128)S(1)}, bf16[8,64,16,256]{3,2,1,0:T(8,128)(2,1)}, bf16[8,64,8,1024]{3,2,1,0:T(8,128)(2,1)}, bf16[1024,1024]{1,0:T(8,128)(2,1)}, /*index=5*/s32[]{:T(128)}, s32[]{:T(128)}) while((s32[]{:T(128)}, f32[8,256,64]{1,2,0:T(8,128)S(1)}, bf16[8,64,16,256]{3,2,1,0:T(8,128)(2,1)}, ...), condition=%wide.region_1.2_spmd.clone, body=%wide.region_0.1_spmd.clone.sunk | while | flops 1342963712 | bytes 12059227 | solution.py:69
  298.9 8.3 %reshape.37 = bf16[64,8,64,16]{3,2,1,0:T(8,128)(2,1)} reshape(bf16[512,1024]{1,0:T(8,128)(2,1)S(1)} %convolution_convert_fusion.2) | data formatting | bytes 2097152 | tf_op jit(solution)/shard_map/while/body/eval_jaxpr/reshape | solution.py:48
  307.2 12.5 %copy.27 = bf16[64,8,64,16]{0,2,3,1:T(8,128)(2,1)S(1)} copy(bf16[64,8,64,16]{3,2,1,0:T(8,128)(2,1)} %reshape.37) | data formatting | bytes 2097152 | tf_op jit(solution)/shard_map/while/body/eval_jaxpr/reshape | solution.py:48
  321.5 3.2 convolution_convert_fusion.2
  324.7 8.3 %reshape.37 = bf16[64,8,64,16]{3,2,1,0:T(8,128)(2,1)} reshape(bf16[512,1024]{1,0:T(8,128)(2,1)S(1)} %convolution_convert_fusion.2) | data formatting | bytes 2097152 | tf_op jit(solution)/shard_map/while/body/eval_jaxpr/reshape | solution.py:48
  333.0 12.5 %copy.27 = bf16[64,8,64,16]{0,2,3,1:T(8,128)(2,1)S(1)} copy(bf16[64,8,64,16]{3,2,1,0:T(8,128)(2,1)} %reshape.37) | data formatting | bytes 2097152 | tf_op jit(solution)/shard_map/while/body/eval_jaxpr/reshape | solution.py:48
  350.6 8.3 %reshape.37 = bf16[64,8,64,16]{3,2,1,0:T(8,128)(2,1)} reshape(bf16[512,1024]{1,0:T(8,128)(2,1)S(1)} %convolution_convert_fusion.2) | data formatting | bytes 2097152 | tf_op jit(solution)/shard_map/while/body/eval_jaxpr/reshape | solution.py:48
  358.8 12.5 %copy.27 = bf16[64,8,64,16]{0,2,3,1:T(8,128)(2,1)S(1)} copy(bf16[64,8,64,16]{3,2,1,0:T(8,128)(2,1)} %reshape.37) | data formatting | bytes 2097152 | tf_op jit(solution)/shard_map/while/body/eval_jaxpr/reshape | solution.py:48
  373.2 3.2 convolution_convert_fusion.2
  376.4 8.3 %reshape.37 = bf16[64,8,64,16]{3,2,1,0:T(8,128)(2,1)} reshape(bf16[512,1024]{1,0:T(8,128)(2,1)S(1)} %convolution_convert_fusion.2) | data formatting | bytes 2097152 | tf_op jit(solution)/shard_map/while/body/eval_jaxpr/reshape | solution.py:48
  384.7 12.5 %copy.27 = bf16[64,8,64,16]{0,2,3,1:T(8,128)(2,1)S(1)} copy(bf16[64,8,64,16]{3,2,1,0:T(8,128)(2,1)} %reshape.37) | data formatting | bytes 2097152 | tf_op jit(solution)/shard_map/while/body/eval_jaxpr/reshape | solution.py:48
  402.3 8.3 %reshape.37 = bf16[64,8,64,16]{3,2,1,0:T(8,128)(2,1)} reshape(bf16[512,1024]{1,0:T(8,128)(2,1)S(1)} %convolution_convert_fusion.2) | data formatting | bytes 2097152 | tf_op jit(solution)/shard_map/while/body/eval_jaxpr/reshape | solution.py:48
  410.5 12.5 %copy.27 = bf16[64,8,64,16]{0,2,3,1:T(8,128)(2,1)S(1)} copy(bf16[64,8,64,16]{3,2,1,0:T(8,128)(2,1)} %reshape.37) | data formatting | bytes 2097152 | tf_op jit(solution)/shard_map/while/body/eval_jaxpr/reshape | solution.py:48
  428.1 8.3 %reshape.37 = bf16[64,8,64,16]{3,2,1,0:T(8,128)(2,1)} reshape(bf16[512,1024]{1,0:T(8,128)(2,1)S(1)} %convolution_convert_fusion.2) | data formatting | bytes 2097152 | tf_op jit(solution)/shard_map/while/body/eval_jaxpr/reshape | solution.py:48
  436.4 12.5 %copy.27 = bf16[64,8,64,16]{0,2,3,1:T(8,128)(2,1)S(1)} copy(bf16[64,8,64,16]{3,2,1,0:T(8,128)(2,1)} %reshape.37) | data formatting | bytes 2097152 | tf_op jit(solution)/shard_map/while/body/eval_jaxpr/reshape | solution.py:48
  453.9 8.3 %reshape.37 = bf16[64,8,64,16]{3,2,1,0:T(8,128)(2,1)} reshape(bf16[512,1024]{1,0:T(8,128)(2,1)S(1)} %convolution_convert_fusion.2) | data formatting | bytes 2097152 | tf_op jit(solution)/shard_map/while/body/eval_jaxpr/reshape | solution.py:48
  462.2 12.5 %copy.27 = bf16[64,8,64,16]{0,2,3,1:T(8,128)(2,1)S(1)} copy(bf16[64,8,64,16]{3,2,1,0:T(8,128)(2,1)} %reshape.37) | data formatting | bytes 2097152 | tf_op jit(solution)/shard_map/while/body/eval_jaxpr/reshape | solution.py:48
  479.8 8.3 %reshape.37 = bf16[64,8,64,16]{3,2,1,0:T(8,128)(2,1)} reshape(bf16[512,1024]{1,0:T(8,128)(2,1)S(1)} %convolution_convert_fusion.2) | data formatting | bytes 2097152 | tf_op jit(solution)/shard_map/while/body/eval_jaxpr/reshape | solution.py:48
  488.0 12.5 %copy.27 = bf16[64,8,64,16]{0,2,3,1:T(8,128)(2,1)S(1)} copy(bf16[64,8,64,16]{3,2,1,0:T(8,128)(2,1)} %reshape.37) | data formatting | bytes 2097152 | tf_op jit(solution)/shard_map/while/body/eval_jaxpr/reshape | solution.py:48
  503.5 22.4 %all_to_all.11 = f32[32,1,4096]{2,1,0:T(1,128)S(1)} all-to-all(f32[32,1,4096]{2,1,0:T(1,128)S(1)} %reshape.34), channel_id=1, replica_groups=mesh['row'=8,'col'=32] {'col'}, dimensions={0} | all-to-all | bytes 1048576 | tf_op jit(solution)/shard_map/all_to_all | solution.py:30
  (41 shorter events, 44.9 us)
Async XLA Ops:
  6.5 0.8 copy-start
  6.5 119.1 %all-gather.3.cloned.1.call-start = ((), (), s32[]{:S(2)}) async-start(), calls=%async_computation.2 | async-start | bytes 4718592 | tf_op jit(solution)/shard_map/all_gather | solution.py:60
  7.3 288.4 %all-gather.5.cloned.1.call-start = ((), (), s32[]{:S(2)}) async-start(), calls=%async_computation.3 | async-start | bytes 9437184 | tf_op jit(solution)/shard_map/all_gather | solution.py:59
Sparse Core Ops, SparseCore 0:
  10.0 115.6 all-gather.2
  128.2 167.4 all-gather.4
where the time goes:
time: 537 us; the launch traced here: 536 us
  waiting for transfers between devices  231 us (43%)
  local copies, waits for them, and re-layouts  185 us (34%)
  blocking collectives  71.6 us (13%)
  matrix products  32 us (6%)
  between operations  13.5 us (3%)
    all_gather x1, waiting for transfers between devices, local(): lax.all_gather(window, 'row', axis=0, tiled=True)  170 us
    reshape x16, local copies, waits for them, and re-layouts, ladder_term(): integrals.astype(jnp.bfloat16)  166 us
    all_gather x1, waiting for transfers between devices, local(): lax.all_gather(amplitudes, 'row', axis=0, tiled=True)  60.1 us
    all_to_all x1, blocking collectives, from_everyone(): lax.all_to_all(jnp.broadcast_to(x[None], (length, *x.shape)), axis, 0, 0,...  49.2 us
    dot_general x8, matrix products, ladder_term(): lax.dot_general(chol_rows.reshape(-1, chol_count), vectors_flat, (((1,),...  25.6 us
    all_to_all x1, blocking collectives, sent_and_summed(): tiles = lax.all_to_all(cut_along(x, dim, length), axis, 0, 0, tiled=True)  22.4 us
  transfers between devices with their start and end apart: 2, of which 2 were waited for; matrix products, arithmetic and copies ran while one was open for 2% of the time, Pallas kernels for 0%

commit v1 on v0

v1 whole, which is shorter than its diff:
```python
import jax
import jax.numpy as jnp
from jax import lax
from jax.experimental import pallas as pl
from jax.experimental.pallas import tpu as pltpu
from jax.sharding import PartitionSpec as P

X, ZH, Y, ZL, CORE = 4, 2, 4, 4, 2
Z = ZH * ZL
COLS = Y * ZL * CORE
PARTIAL = jnp.bfloat16
GROUPS = ((0, 1, 7), (2, 6, 3, 5, 4))


def linear(x, zh, y, zl, core):
    return (((x % X * ZH + zh % ZH) * Y + y % Y) * ZL + zl % ZL) * CORE + core % CORE


def fetch(array, dx=0, dy=0, dz=0, dcore=0):
    perm = []
    for x in range(X):
        for z in range(Z):
            for y in range(Y):
                for core in range(CORE):
                    far = (z + dz) % Z
                    perm.append((
                        linear(x + dx, far // ZL, y + dy, far % ZL, core + dcore),
                        linear(x, z // ZL, y, z % ZL, core),
                    ))
    return lax.ppermute(array, ("row", "col"), perm)


def place():
    row, col = lax.axis_index("row"), lax.axis_index("col")
    return lax.rem(row, ZH), col // (ZL * CORE), lax.rem(col // CORE, ZL), lax.rem(col, CORE)


def integrals_kernel(*refs):
    pieces, (vectors_ref, out_ref) = refs[:-2], refs[-2:]
    zh, _, zl, _ = place()
    swapped = [lax.rem((zh * ZL + zl + step) // ZL, ZH) != 0 for step in range(ZL)]
    rows = []
    for pair in range(CORE * Y):
        held = {}
        for g, group in enumerate(GROUPS):
            for i, dz in enumerate(group):
                held[dz] = pieces[pair * len(GROUPS) + g][i, 0]
        for step in range(ZL):
            near, far = held[step], held[step + ZL]
            low = jnp.where(swapped[step], far, near)
            high = jnp.where(swapped[step], near, far)
            rows.append(jnp.concatenate([low, high], axis=1))
    window = jnp.concatenate(rows, axis=0)
    block = jnp.dot(vectors_ref[...], window, preferred_element_type=jnp.float32)
    out_ref[...] = block.astype(out_ref.dtype)


def integrals_of(pieces, vectors):
    _, n_a, q_own, c_half = pieces[0].shape
    rows, n_q = vectors.shape
    n_c = c_half * ZH
    specs = [
        pl.BlockSpec((piece.shape[0], 1, q_own, c_half), lambda a: (0, a, 0, 0)) for piece in pieces
    ]
    return pl.pallas_call(
        integrals_kernel,
        grid=(n_a,),
        out_shape=jax.ShapeDtypeStruct((rows, n_a * n_c), jnp.bfloat16),
        in_specs=specs + [pl.BlockSpec((rows, n_q), lambda a: (0, 0))],
        out_specs=pl.BlockSpec((rows, n_c), lambda a: (0, a)),
        compiler_params=pltpu.CompilerParams(vmem_limit_bytes=24 << 20),
        cost_estimate=pl.CostEstimate(
            flops=2 * rows * n_q * n_a * n_c, transcendentals=0,
            bytes_accessed=2 * (n_q * n_a * n_c + rows * n_q + rows * n_a * n_c),
        ),
    )(*pieces, vectors)


def ladder_kernel(*refs, n_a, n_b, n_c, d_block):
    amps, (integrals_ref, out_ref, acc_ref) = refs[:-3], refs[-3:]
    zh = place()[0]
    block = pl.program_id(0)

    @pl.when(block == 0)
    def _():
        acc_ref[...] = jnp.zeros_like(acc_ref)

    total = acc_ref[...]
    for d in range(d_block):
        near = jnp.concatenate([amps[i][d] for i in range(X)], axis=0)
        far = jnp.concatenate([amps[X + i][d] for i in range(X)], axis=0)
        low, high = jnp.where(zh != 0, far, near), jnp.where(zh != 0, near, far)
        amplitudes = jnp.concatenate([low, high], axis=0)
        stacked = jnp.concatenate(
            [integrals_ref[d * n_b:(d + 1) * n_b, a * n_c:(a + 1) * n_c] for a in range(n_a)], axis=0)
        total += jnp.dot(stacked, amplitudes, preferred_element_type=jnp.float32)
    acc_ref[...] = total

    @pl.when(block == pl.num_programs(0) - 1)
    def _():
        out_ref[...] = acc_ref[...].T.astype(out_ref.dtype)


def ladder_of(integrals, amps, n_a, d_block=4):
    n_d, c_own, n_n = amps[0].shape
    n_c = c_own * X * ZH
    n_b = integrals.shape[0] // n_d

    def kernel(*refs):
        ladder_kernel(*refs, n_a=n_a, n_b=n_b, n_c=n_c, d_block=d_block)

    return pl.pallas_call(
        kernel,
        grid=(n_d // d_block,),
        out_shape=jax.ShapeDtypeStruct((n_n, n_a * n_b), PARTIAL),
        in_specs=[pl.BlockSpec((d_block, c_own, n_n), lambda d: (d, 0, 0))] * len(amps)
        + [pl.BlockSpec((d_block * n_b, n_a * n_c), lambda d: (d, 0))],
        out_specs=pl.BlockSpec((n_n, n_a * n_b), lambda d: (0, 0)),
        scratch_shapes=[pltpu.VMEM((n_a * n_b, n_n), jnp.float32)],
        compiler_params=pltpu.CompilerParams(vmem_limit_bytes=24 << 20),
        cost_estimate=pl.CostEstimate(
            flops=2 * n_d * n_b * n_a * n_c * n_n, transcendentals=0,
            bytes_accessed=2 * (n_d * n_c * n_n + n_d * n_b * n_a * n_c),
        ),
    )(*amps, integrals)


def ordered_vectors(pair_vectors):
    n_b, n_d, n_q = pair_vectors.shape
    _, y, zl, core = place()
    own = n_q // COLS
    position = jnp.arange(n_q)
    far, q = position // own, position % own
    dzl, dy, dcore = far % ZL, far // ZL % Y, far // (ZL * Y)
    source = (((y + dy) % Y * ZL + (zl + dzl) % ZL) * CORE + (core + dcore) % CORE) * own + q
    picked = (jnp.arange(n_q)[:, None] == source[None, :]).astype(pair_vectors.dtype)
    moved = pair_vectors.transpose(1, 0, 2).reshape(n_d * n_b, n_q)
    return jnp.dot(moved, picked, preferred_element_type=jnp.float32).astype(pair_vectors.dtype)


def gathered_window(window):
    mine = window.transpose(1, 2, 0)
    near = [mine] + [fetch(mine, dx=dx) for dx in range(1, X)]
    parts = jnp.concatenate(near, axis=2)
    along_z = [parts] + [fetch(parts, dz=dz) for dz in range(1, Z)]
    groups = [jnp.stack([along_z[dz] for dz in group]) for group in GROUPS]
    along_y = [[group] + [fetch(group, dy=dy) for dy in range(1, Y)] for group in groups]
    both = [along_y] + [[[fetch(part, dcore=1) for part in parts_y] for parts_y in along_y]]
    return [both[dcore][g][dy] for dcore in range(CORE) for dy in range(Y) for g in range(len(GROUPS))]


def local(chol_window, pair_vectors, amplitudes):
    n_b = pair_vectors.shape[0]
    n_a = chol_window.shape[1]
    n_n = amplitudes.shape[2]
    pieces = gathered_window(chol_window)
    amps_mine = amplitudes.transpose(1, 0, 2)
    amps_near = [amps_mine] + [fetch(amps_mine, dx=dx) for dx in range(1, X)]
    amps_swap = fetch(amps_mine, dz=ZL)
    amps_far = [amps_swap] + [fetch(amps_swap, dx=dx) for dx in range(1, X)]
    integrals = integrals_of(pieces, ordered_vectors(pair_vectors))
    partial = ladder_of(integrals, amps_near + amps_far, n_a)
    tiles = lax.all_to_all(partial.reshape(COLS, n_n // COLS, n_a * n_b), "col", 0, 0, tiled=True)
    total = jnp.sum(tiles.astype(jnp.float32), axis=0)
    return total.reshape(n_n // COLS, n_a, n_b).transpose(1, 0, 2)


def solution(mesh):
    return jax.shard_map(
        local,
        mesh=mesh,
        in_specs=(P("row", None, "col"), P("row", "col", None), P("row", "col", None)),
        out_specs=P(None, "col", "row"),
        check_vma=False,
    )
```

time: 537 us -> 198 us (0.37)
  local copies, waits for them, and re-layouts: 185 us -> 6.87 us
  waiting for transfers between devices: 231 us -> 81.8 us
  starting transfers between devices: 0.04 us -> 68.9 us
  blocking collectives: 71.6 us -> 18.8 us
  matrix products: 32 us -> 4.09 us
  Pallas kernels: 0 us -> 16 us
  between operations: 13.5 us -> 0.16 us
    all_gather x2 -> x0, waiting for transfers between devices: 230 us -> none  [the longest x1 170 us: local(): lax.all_gather(window, 'row', axis=0, tiled=True)]
    reshape x17 -> x1, local copies, waits for them, and re-layouts: 168 us -> 0.08 us  [local(): return total.reshape(n_n // COLS, n_a, n_b).transpose(1, 0, 2)]
    ppermute x0 -> x31, waiting for transfers between devices: none -> 81.8 us  [fetch(): return lax.ppermute(array, ('row', 'col'), perm)]
    ppermute x0 -> x31, starting transfers between devices: none -> 68.9 us  [fetch(): return lax.ppermute(array, ('row', 'col'), perm)]
    all_to_all x2 -> x1, blocking collectives: 71.6 us -> 18.8 us  [local(): lax.all_to_all(partial.reshape(COLS, n_n // COLS, n_a * n_b), 'col', 0, 0...]
    dot_general x16 -> x1, matrix products: 32 us -> 4.09 us  [ordered_vectors(): jnp.dot(moved, picked, preferred_element_type=jnp.float32)]
    pallas_call x0 -> x2, Pallas kernels: none -> 16 us  [the longest x1 12.9 us: integrals_of(): pl.pallas_call(integrals_kernel, grid=(n_a,), out_shape=jax.ShapeDtypeStr...]
    dynamic_slice x8 -> x0, local copies, waits for them, and re-layouts: 8.66 us -> none  [local(): running, unused = lax.scan(scan_step, running, (chol_blocks, amp_blocks))]
  transfers between devices with their start and end apart: 2 -> 31, of which waited for: 2 -> 12; matrix products, arithmetic and copies ran while one was open for 2% -> 5% of each run, Pallas kernels for 0% -> 7%
where the time goes in v1:
time: 198 us
  waiting for transfers between devices  81.8 us (41%)
  starting transfers between devices  68.9 us (35%)
  blocking collectives  18.8 us (9%)
  Pallas kernels  16 us (8%)
  local copies, waits for them, and re-layouts  6.87 us (3%)
  matrix products  4.09 us (2%)
    ppermute x31, waiting for transfers between devices, fetch(): return lax.ppermute(array, ('row', 'col'), perm)  81.8 us
    ppermute x31, starting transfers between devices, fetch(): return lax.ppermute(array, ('row', 'col'), perm)  68.9 us
    all_to_all x1, blocking collectives, local(): lax.all_to_all(partial.reshape(COLS, n_n // COLS, n_a * n_b), 'col', 0, 0...  18.8 us
    pallas_call x1, Pallas kernels, integrals_of(): pl.pallas_call(integrals_kernel, grid=(n_a,), out_shape=jax.ShapeDtypeStr...  12.9 us
    unnamed x18, local copies, waits for them, and re-layouts  6.15 us
    dot_general x1, matrix products, ordered_vectors(): jnp.dot(moved, picked, preferred_element_type=jnp.float32)  4.09 us
  transfers between devices with their start and end apart: 31, of which 12 were waited for; matrix products, arithmetic and copies ran while one was open for 5% of the time, Pallas kernels for 7%

profile of v1, /device:TPU:1, one launch (start us, length us, event | category | flops | bytes accessed | tf_op | source)
XLA Modules:
  0.0 197.8 jit_solution(9351105770622456728)
XLA Ops:
  0.0 3.3 %collective-permute-start.7 = (bf16[8,32,64]{2,1,0:T(8,128)(2,1)}, bf16[8,32,64]{2,1,0:T(8,128)(2,1)S(1)}, u32[]{:S(2)}, u32[]{:S(2)}) collective-permute-start(bf16[8,32,64]{2,1,0:T(8,128)(2,1)} %bitcast.36), channel_id=1, source_target_pairs={{64,0},{65,1},{72,8},{73,9},{80,16},{81,17},{88,24},{89,25},{66,2}... | collective-permute-start | bytes 98312 | tf_op jit(solution)/shard_map/ppermute | solution.py:30
  4.9 3.2 %collective-permute-done.8 = bf16[8,32,64]{2,1,0:T(8,128)(2,1)S(1)} collective-permute-done((bf16[8,32,64]{2,1,0:T(8,128)(2,1)}, bf16[8,32,64]{2,1,0:T(8,128)(2,1)S(1)}, u32[]{:S(2)}, u32[]{:S(2)}) %collective-permute-start.8) | collective-permute-done | bytes 32800 | tf_op jit(solution)/shard_map/ppermute | solution.py:30
  9.8 6.1 %collective-permute-start.12 = (bf16[8,32,256]{2,1,0:T(8,128)(2,1)S(1)}, bf16[8,32,256]{2,1,0:T(8,128)(2,1)S(1)}, u32[]{:S(2)}, u32[]{:S(2)}) collective-permute-start(bf16[8,32,256]{2,1,0:T(8,128)(2,1)S(1)} %pad_maximum_fusion.1), channel_id=1, source_target_pairs={{4,0},{5,1},{12,8},{13,9},{20,16},{21,17},{28,24},{29,25},{6,2},{7... | collective-permute-start | bytes 393224 | tf_op jit(solution)/shard_map/ppermute | solution.py:30
  23.4 20.8 %collective-permute-done.13 = bf16[8,32,256]{2,1,0:T(8,128)(2,1)S(1)} collective-permute-done((bf16[8,32,256]{2,1,0:T(8,128)(2,1)S(1)}, bf16[8,32,256]{2,1,0:T(8,128)(2,1)S(1)}, u32[]{:S(2)}, u32[]{:S(2)}) %collective-permute-start.13) | collective-permute-done | bytes 131104 | tf_op jit(solution)/shard_map/ppermute | solution.py:30
  44.2 4.6 %collective-permute-start.11 = (bf16[8,32,256]{2,1,0:T(8,128)(2,1)S(1)}, bf16[8,32,256]{2,1,0:T(8,128)(2,1)S(1)}, u32[]{:S(2)}, u32[]{:S(2)}) collective-permute-start(bf16[8,32,256]{2,1,0:T(8,128)(2,1)S(1)} %pad_maximum_fusion.1), channel_id=1, source_target_pairs={{38,0},{39,1},{46,8},{47,9},{54,16},{55,17},{62,24},{63,25},{0,2},... | collective-permute-start | bytes 393224 | tf_op jit(solution)/shard_map/ppermute | solution.py:30
  48.8 5.7 %collective-permute-done.10 = bf16[8,32,256]{2,1,0:T(8,128)(2,1)S(1)} collective-permute-done((bf16[8,32,256]{2,1,0:T(8,128)(2,1)S(1)}, bf16[8,32,256]{2,1,0:T(8,128)(2,1)S(1)}, u32[]{:S(2)}, u32[]{:S(2)}) %collective-permute-start.10) | collective-permute-done | bytes 131104 | tf_op jit(solution)/shard_map/ppermute | solution.py:30
  54.6 3.6 %collective-permute-start.15 = (bf16[8,32,256]{2,1,0:T(8,128)(2,1)S(1)}, bf16[8,32,256]{2,1,0:T(8,128)(2,1)S(1)}, u32[]{:S(2)}, u32[]{:S(2)}) collective-permute-start(bf16[8,32,256]{2,1,0:T(8,128)(2,1)S(1)} %pad_maximum_fusion.1), channel_id=1, source_target_pairs={{34,0},{35,1},{42,8},{43,9},{50,16},{51,17},{58,24},{59,25},{36,2}... | collective-permute-start | bytes 393224 | tf_op jit(solution)/shard_map/ppermute | solution.py:30
  61.0 2.8 %collective-permute-start.17 = (bf16[3,8,32,256]{3,2,1,0:T(8,128)(2,1)S(1)}, bf16[3,8,32,256]{3,2,1,0:T(8,128)(2,1)}, u32[]{:S(2)}, u32[]{:S(2)}) collective-permute-start(bf16[3,8,32,256]{3,2,1,0:T(8,128)(2,1)S(1)} %pad_maximum_fusion.refs_0_), channel_id=1, source_target_pairs={{8,0},{9,1},{16,8},{17,9},{24,16},{25,17},{0,24},{1,25},{10,2},{11... | collective-permute-start | bytes 1179656 | tf_op jit(solution)/shard_map/ppermute | solution.py:30
  63.8 3.1 %collective-permute-done.15 = bf16[8,32,256]{2,1,0:T(8,128)(2,1)S(1)} collective-permute-done((bf16[8,32,256]{2,1,0:T(8,128)(2,1)S(1)}, bf16[8,32,256]{2,1,0:T(8,128)(2,1)S(1)}, u32[]{:S(2)}, u32[]{:S(2)}) %collective-permute-start.15) | collective-permute-done | bytes 131104 | tf_op jit(solution)/shard_map/ppermute | solution.py:30
  66.9 2.9 %collective-permute-start.19 = (bf16[3,8,32,256]{3,2,1,0:T(8,128)(2,1)S(1)}, bf16[3,8,32,256]{3,2,1,0:T(8,128)(2,1)S(1)}, u32[]{:S(2)}, u32[]{:S(2)}) collective-permute-start(bf16[3,8,32,256]{3,2,1,0:T(8,128)(2,1)S(1)} %pad_maximum_fusion.refs_0_), channel_id=1, source_target_pairs={{16,0},{17,1},{24,8},{25,9},{0,16},{1,17},{8,24},{9,25},{18,2},{19... | collective-permute-start | bytes 1179656 | tf_op jit(solution)/shard_map/ppermute | solution.py:30
  69.8 4.1 %collective-permute-done.16 = bf16[8,32,256]{2,1,0:T(8,128)(2,1)S(1)} collective-permute-done((bf16[8,32,256]{2,1,0:T(8,128)(2,1)S(1)}, bf16[8,32,256]{2,1,0:T(8,128)(2,1)S(1)}, u32[]{:S(2)}, u32[]{:S(2)}) %collective-permute-start.16) | collective-permute-done | bytes 131104 | tf_op jit(solution)/shard_map/ppermute | solution.py:30
  78.8 4.4 %collective-permute-start.23 = (bf16[3,8,32,256]{3,2,1,0:T(8,128)(2,1)S(1)}, bf16[3,8,32,256]{3,2,1,0:T(8,128)(2,1)S(1)}, u32[]{:S(2)}, u32[]{:S(2)}) collective-permute-start(bf16[3,8,32,256]{3,2,1,0:T(8,128)(2,1)S(1)} %pad_maximum_fusion.refs_0_), channel_id=1, source_target_pairs={{1,0},{0,1},{9,8},{8,9},{17,16},{16,17},{25,24},{24,25},{3,2},{2,3... | collective-permute-start | bytes 1179656 | tf_op jit(solution)/shard_map/ppermute | solution.py:30
  83.2 5.5 %collective-permute-done.21.refs_6_ = bf16[3,8,32,256]{3,2,1,0:T(8,128)(2,1)S(1)} collective-permute-done((bf16[3,8,32,256]{3,2,1,0:T(8,128)(2,1)S(1)}, bf16[3,8,32,256]{3,2,1,0:T(8,128)(2,1)S(1)}, u32[]{:S(2)}, u32[]{:S(2)}) %collective-permute-start.21) | collective-permute-done | bytes 393248 | tf_op jit(solution)/shard_map/ppermute | solution.py:30
  88.7 13.9 %collective-permute-start.24 = (bf16[5,8,32,256]{3,2,1,0:T(8,128)(2,1)S(1)}, bf16[5,8,32,256]{3,2,1,0:T(8,128)(2,1)}, u32[]{:S(2)}, u32[]{:S(2)}) collective-permute-start(bf16[5,8,32,256]{3,2,1,0:T(8,128)(2,1)S(1)} %bitcast_dynamic-update-slice_fusion.refs_1_), channel_id=1, source_target_pairs={{1,0},{0,1},{9,8},{8,9},{17,16},{16,17},{25,24},{24,25},{3,2},{2,3... | collective-permute-start | bytes 1966088 | tf_op jit(solution)/shard_map/ppermute | solution.py:30
  103.5 6.2 %collective-permute-start.26 = (bf16[5,8,32,256]{3,2,1,0:T(8,128)(2,1)S(1)}, bf16[5,8,32,256]{3,2,1,0:T(8,128)(2,1)}, u32[]{:S(2)}, u32[]{:S(2)}) collective-permute-start(bf16[5,8,32,256]{3,2,1,0:T(8,128)(2,1)S(1)} %collective-permute-done.18.refs_3_), channel_id=1, source_target_pairs={{1,0},{0,1},{9,8},{8,9},{17,16},{16,17},{25,24},{24,25},{3,2},{2,3... | collective-permute-start | bytes 1966088 | tf_op jit(solution)/shard_map/ppermute | solution.py:30
  109.7 6.5 %collective-permute-done.22.refs_7_ = bf16[5,8,32,256]{3,2,1,0:T(8,128)(2,1)} collective-permute-done((bf16[5,8,32,256]{3,2,1,0:T(8,128)(2,1)S(1)}, bf16[5,8,32,256]{3,2,1,0:T(8,128)(2,1)}, u32[]{:S(2)}, u32[]{:S(2)}) %collective-permute-start.22) | collective-permute-done | bytes 655392 | tf_op jit(solution)/shard_map/ppermute | solution.py:30
  117.1 4.1 %copy.7 = bf16[64,16,1024]{2,0,1:T(8,128)(2,1)} copy(bf16[64,16,1024]{2,1,0:T(8,128)(2,1)} %param.4) | data formatting | bytes 4194304 | tf_op args[1]
  121.8 4.1 %convert_bitcast_fusion.refs_16_ = bf16[1024,1024]{1,0:T(8,128)(2,1)S(1)} fusion(bf16[1024,1024]{1,0:T(8,128)(2,1)} %bitcast.31, s32[1024]{0:T(1024)S(1)} %fusion.16), kind=kOutput, calls=%fused_computation.2 | convolution fusion | flops 2149580800 | bytes 4198400 | tf_op jit(solution)/shard_map/dot_general | solution.py:138
  130.5 12.9 %shard_map.37.refs_8_ = bf16[1024,4096]{1,0:T(8,128)(2,1)S(1)} custom-call(bf16[3,8,32,256]{3,2,1,0:T(8,128)(2,1)S(1)} %pad_maximum_fusion.refs_0_, bf16[5,8,32,256]{3,2,1,0:T(8,128)(2,1)S(1)} %bitcast_dynamic-update-slice_fusion.refs_1_, bf16[3,8,32,256]{3,2,1,0:T(8,128)(2,1)} %collective-permute-done.17.refs_2_, ...), custom_call_target="tpu_custom_call" | custom-call | flops 8589934592 | bytes 18874368 | tf_op jit(solution)/shard_map/pallas_call | solution.py:65
  143.5 9.6 %collective-permute-done.2.refs_3_ = bf16[16,64,256]{2,1,0:T(8,128)(2,1)S(1)} collective-permute-done((bf16[16,64,256]{2,1,0:T(8,128)(2,1)S(1)}, bf16[16,64,256]{2,1,0:T(8,128)(2,1)S(1)}, u32[]{:S(2)}, u32[]{:S(2)}) %collective-permute-start.2) | collective-permute-done | bytes 524320 | tf_op jit(solution)/shard_map/ppermute | solution.py:30
  153.1 10.4 %collective-permute-done.5.refs_6_ = bf16[16,64,256]{2,1,0:T(8,128)(2,1)S(1)} collective-permute-done((bf16[16,64,256]{2,1,0:T(8,128)(2,1)S(1)}, bf16[16,64,256]{2,1,0:T(8,128)(2,1)S(1)}, u32[]{:S(2)}, u32[]{:S(2)}) %collective-permute-start.5) | collective-permute-done | bytes 524320 | tf_op jit(solution)/shard_map/ppermute | solution.py:30
  163.4 11.6 %collective-permute-done.6.refs_7_ = bf16[16,64,256]{2,1,0:T(8,128)(2,1)S(1)} collective-permute-done((bf16[16,64,256]{2,1,0:T(8,128)(2,1)S(1)}, bf16[16,64,256]{2,1,0:T(8,128)(2,1)S(1)}, u32[]{:S(2)}, u32[]{:S(2)}) %collective-permute-start.6) | collective-permute-done | bytes 524320 | tf_op jit(solution)/shard_map/ppermute | solution.py:30
  175.1 3.1 %shard_map.38 = bf16[256,512]{1,0:T(8,128)(2,1)S(1)} custom-call(bf16[16,64,256]{2,1,0:T(8,128)(2,1)S(1)} %bitcast.29, bf16[16,64,256]{2,1,0:T(8,128)(2,1)S(1)} %collective-permute-done.refs_1_, bf16[16,64,256]{2,1,0:T(8,128)(2,1)S(1)} %collective-permute-done.1.refs_2_, bf16[16,64,256]{2,1,0:T(8,128)(2,1)S(1)} %collective-permute-done.2.refs_3_, ...), custom_call_target="tpu_custom_call" | custom-call | flops 2147483648 | bytes 12582912 | tf_op jit(solution)/shard_map/pallas_call | solution.py:112
  178.2 18.8 %all_to_all.5 = bf16[32,8,512]{2,1,0:T(8,128)(2,1)S(1)} all-to-all(bf16[32,8,512]{2,1,0:T(8,128)(2,1)S(1)} %bitcast.30), channel_id=1, replica_groups=mesh['row'=8,'col'=32] {'col'}, dimensions={0} | all-to-all | bytes 524288 | tf_op jit(solution)/shard_map/all_to_all | solution.py:163
  (67 shorter events, 26.1 us)
Async XLA Ops:
  9.8 12.9 %collective-permute-start.12 = (bf16[8,32,256]{2,1,0:T(8,128)(2,1)S(1)}, bf16[8,32,256]{2,1,0:T(8,128)(2,1)S(1)}, u32[]{:S(2)}, u32[]{:S(2)}) collective-permute-start(bf16[8,32,256]{2,1,0:T(8,128)(2,1)S(1)} %pad_maximum_fusion.1), channel_id=1, source_target_pairs={{4,0},{5,1},{12,8},{13,9},{20,16},{21,17},{28,24},{29,25},{6,2},{7... | collective-permute-start | bytes 393224 | tf_op jit(solution)/shard_map/ppermute | solution.py:30
  17.1 58.1 %collective-permute-start.3 = (bf16[16,64,256]{2,1,0:T(8,128)(2,1)S(1)}, bf16[16,64,256]{2,1,0:T(8,128)(2,1)S(1)}, u32[]{:S(2)}, u32[]{:S(2)}) collective-permute-start(bf16[16,64,256]{2,1,0:T(8,128)(2,1)S(1)} %bitcast.25), channel_id=1, source_target_pairs={{32,0},{33,1},{40,8},{41,9},{48,16},{49,17},{56,24},{57,25},{34,2}... | collective-permute-start | bytes 1572872 | tf_op jit(solution)/shard_map/ppermute | solution.py:30
  18.1 58.7 %collective-permute-start = (bf16[16,64,256]{2,1,0:T(8,128)(2,1)S(1)}, bf16[16,64,256]{2,1,0:T(8,128)(2,1)S(1)}, u32[]{:S(2)}, u32[]{:S(2)}) collective-permute-start(bf16[16,64,256]{2,1,0:T(8,128)(2,1)S(1)} %bitcast.26), channel_id=1, source_target_pairs={{64,0},{65,1},{72,8},{73,9},{80,16},{81,17},{88,24},{89,25},{66,2}... | collective-permute-start | bytes 1572872 | tf_op jit(solution)/shard_map/ppermute | solution.py:30
  18.7 25.6 %collective-permute-start.13 = (bf16[8,32,256]{2,1,0:T(8,128)(2,1)S(1)}, bf16[8,32,256]{2,1,0:T(8,128)(2,1)S(1)}, u32[]{:S(2)}, u32[]{:S(2)}) collective-permute-start(bf16[8,32,256]{2,1,0:T(8,128)(2,1)S(1)} %pad_maximum_fusion.1), channel_id=1, source_target_pairs={{36,0},{37,1},{44,8},{45,9},{52,16},{53,17},{60,24},{61,25},{38,2}... | collective-permute-start | bytes 393224 | tf_op jit(solution)/shard_map/ppermute | solution.py:30
  21.0 40.0 %collective-permute-start.14 = (bf16[8,32,256]{2,1,0:T(8,128)(2,1)S(1)}, bf16[8,32,256]{2,1,0:T(8,128)(2,1)S(1)}, u32[]{:S(2)}, u32[]{:S(2)}) collective-permute-start(bf16[8,32,256]{2,1,0:T(8,128)(2,1)S(1)} %pad_maximum_fusion.1), channel_id=1, source_target_pairs={{6,0},{7,1},{14,8},{15,9},{22,16},{23,17},{30,24},{31,25},{32,2},{... | collective-permute-start | bytes 393224 | tf_op jit(solution)/shard_map/ppermute | solution.py:30
  22.7 31.9 %collective-permute-start.10 = (bf16[8,32,256]{2,1,0:T(8,128)(2,1)S(1)}, bf16[8,32,256]{2,1,0:T(8,128)(2,1)S(1)}, u32[]{:S(2)}, u32[]{:S(2)}) collective-permute-start(bf16[8,32,256]{2,1,0:T(8,128)(2,1)S(1)} %pad_maximum_fusion.1), channel_id=1, source_target_pairs={{2,0},{3,1},{10,8},{11,9},{18,16},{19,17},{26,24},{27,25},{4,2},{5... | collective-permute-start | bytes 393224 | tf_op jit(solution)/shard_map/ppermute | solution.py:30
  44.2 14.0 %collective-permute-start.11 = (bf16[8,32,256]{2,1,0:T(8,128)(2,1)S(1)}, bf16[8,32,256]{2,1,0:T(8,128)(2,1)S(1)}, u32[]{:S(2)}, u32[]{:S(2)}) collective-permute-start(bf16[8,32,256]{2,1,0:T(8,128)(2,1)S(1)} %pad_maximum_fusion.1), channel_id=1, source_target_pairs={{38,0},{39,1},{46,8},{47,9},{54,16},{55,17},{62,24},{63,25},{0,2},... | collective-permute-start | bytes 393224 | tf_op jit(solution)/shard_map/ppermute | solution.py:30
  58.2 15.7 %collective-permute-start.16 = (bf16[8,32,256]{2,1,0:T(8,128)(2,1)S(1)}, bf16[8,32,256]{2,1,0:T(8,128)(2,1)S(1)}, u32[]{:S(2)}, u32[]{:S(2)}) collective-permute-start(bf16[8,32,256]{2,1,0:T(8,128)(2,1)S(1)} %pad_maximum_fusion.1), channel_id=1, source_target_pairs={{32,0},{33,1},{40,8},{41,9},{48,16},{49,17},{56,24},{57,25},{34,2}... | collective-permute-start | bytes 393224 | tf_op jit(solution)/shard_map/ppermute | solution.py:30
  61.0 17.4 %collective-permute-start.17 = (bf16[3,8,32,256]{3,2,1,0:T(8,128)(2,1)S(1)}, bf16[3,8,32,256]{3,2,1,0:T(8,128)(2,1)}, u32[]{:S(2)}, u32[]{:S(2)}) collective-permute-start(bf16[3,8,32,256]{3,2,1,0:T(8,128)(2,1)S(1)} %pad_maximum_fusion.refs_0_), channel_id=1, source_target_pairs={{8,0},{9,1},{16,8},{17,9},{24,16},{25,17},{0,24},{1,25},{10,2},{11... | collective-permute-start | bytes 1179656 | tf_op jit(solution)/shard_map/ppermute | solution.py:30
  73.9 14.8 %collective-permute-start.21 = (bf16[3,8,32,256]{3,2,1,0:T(8,128)(2,1)S(1)}, bf16[3,8,32,256]{3,2,1,0:T(8,128)(2,1)S(1)}, u32[]{:S(2)}, u32[]{:S(2)}) collective-permute-start(bf16[3,8,32,256]{3,2,1,0:T(8,128)(2,1)S(1)} %pad_maximum_fusion.refs_0_), channel_id=1, source_target_pairs={{24,0},{25,1},{0,8},{1,9},{8,16},{9,17},{16,24},{17,25},{26,2},{27... | collective-permute-start | bytes 1179656 | tf_op jit(solution)/shard_map/ppermute | solution.py:30
  75.2 28.2 %collective-permute-start.18 = (bf16[5,8,32,256]{3,2,1,0:T(8,128)(2,1)S(1)}, bf16[5,8,32,256]{3,2,1,0:T(8,128)(2,1)S(1)}, u32[]{:S(2)}, u32[]{:S(2)}) collective-permute-start(bf16[5,8,32,256]{3,2,1,0:T(8,128)(2,1)S(1)} %bitcast_dynamic-update-slice_fusion.refs_1_), channel_id=1, source_target_pairs={{8,0},{9,1},{16,8},{17,9},{24,16},{25,17},{0,24},{1,25},{10,2},{11... | collective-permute-start | bytes 1966088 | tf_op jit(solution)/shard_map/ppermute | solution.py:30
  76.8 32.9 %collective-permute-start.20 = (bf16[5,8,32,256]{3,2,1,0:T(8,128)(2,1)S(1)}, bf16[5,8,32,256]{3,2,1,0:T(8,128)(2,1)}, u32[]{:S(2)}, u32[]{:S(2)}) collective-permute-start(bf16[5,8,32,256]{3,2,1,0:T(8,128)(2,1)S(1)} %bitcast_dynamic-update-slice_fusion.refs_1_), channel_id=1, source_target_pairs={{16,0},{17,1},{24,8},{25,9},{0,16},{1,17},{8,24},{9,25},{18,2},{19... | collective-permute-start | bytes 1966088 | tf_op jit(solution)/shard_map/ppermute | solution.py:30
  78.4 37.8 %collective-permute-start.22 = (bf16[5,8,32,256]{3,2,1,0:T(8,128)(2,1)S(1)}, bf16[5,8,32,256]{3,2,1,0:T(8,128)(2,1)}, u32[]{:S(2)}, u32[]{:S(2)}) collective-permute-start(bf16[5,8,32,256]{3,2,1,0:T(8,128)(2,1)S(1)} %bitcast_dynamic-update-slice_fusion.refs_1_), channel_id=1, source_target_pairs={{24,0},{25,1},{0,8},{1,9},{8,16},{9,17},{16,24},{17,25},{26,2},{27... | collective-permute-start | bytes 1966088 | tf_op jit(solution)/shard_map/ppermute | solution.py:30
  78.8 23.8 %collective-permute-start.23 = (bf16[3,8,32,256]{3,2,1,0:T(8,128)(2,1)S(1)}, bf16[3,8,32,256]{3,2,1,0:T(8,128)(2,1)S(1)}, u32[]{:S(2)}, u32[]{:S(2)}) collective-permute-start(bf16[3,8,32,256]{3,2,1,0:T(8,128)(2,1)S(1)} %pad_maximum_fusion.refs_0_), channel_id=1, source_target_pairs={{1,0},{0,1},{9,8},{8,9},{17,16},{16,17},{25,24},{24,25},{3,2},{2,3... | collective-permute-start | bytes 1179656 | tf_op jit(solution)/shard_map/ppermute | solution.py:30
  88.7 32.5 %collective-permute-start.24 = (bf16[5,8,32,256]{3,2,1,0:T(8,128)(2,1)S(1)}, bf16[5,8,32,256]{3,2,1,0:T(8,128)(2,1)}, u32[]{:S(2)}, u32[]{:S(2)}) collective-permute-start(bf16[5,8,32,256]{3,2,1,0:T(8,128)(2,1)S(1)} %bitcast_dynamic-update-slice_fusion.refs_1_), channel_id=1, source_target_pairs={{1,0},{0,1},{9,8},{8,9},{17,16},{16,17},{25,24},{24,25},{3,2},{2,3... | collective-permute-start | bytes 1966088 | tf_op jit(solution)/shard_map/ppermute | solution.py:30
  103.4 17.9 %collective-permute-start.25 = (bf16[3,8,32,256]{3,2,1,0:T(8,128)(2,1)}, bf16[3,8,32,256]{3,2,1,0:T(8,128)(2,1)}, u32[]{:S(2)}, u32[]{:S(2)}) collective-permute-start(bf16[3,8,32,256]{3,2,1,0:T(8,128)(2,1)} %collective-permute-done.17.refs_2_), channel_id=1, source_target_pairs={{1,0},{0,1},{9,8},{8,9},{17,16},{16,17},{25,24},{24,25},{3,2},{2,3... | collective-permute-start | bytes 1179656 | tf_op jit(solution)/shard_map/ppermute | solution.py:30
  103.5 23.4 %collective-permute-start.26 = (bf16[5,8,32,256]{3,2,1,0:T(8,128)(2,1)S(1)}, bf16[5,8,32,256]{3,2,1,0:T(8,128)(2,1)}, u32[]{:S(2)}, u32[]{:S(2)}) collective-permute-start(bf16[5,8,32,256]{3,2,1,0:T(8,128)(2,1)S(1)} %collective-permute-done.18.refs_3_), channel_id=1, source_target_pairs={{1,0},{0,1},{9,8},{8,9},{17,16},{16,17},{25,24},{24,25},{3,2},{2,3... | collective-permute-start | bytes 1966088 | tf_op jit(solution)/shard_map/ppermute | solution.py:30
  109.7 19.9 %collective-permute-start.28 = (bf16[5,8,32,256]{3,2,1,0:T(8,128)(2,1)}, bf16[5,8,32,256]{3,2,1,0:T(8,128)(2,1)}, u32[]{:S(2)}, u32[]{:S(2)}) collective-permute-start(bf16[5,8,32,256]{3,2,1,0:T(8,128)(2,1)} %collective-permute-done.20.refs_5_), channel_id=1, source_target_pairs={{1,0},{0,1},{9,8},{8,9},{17,16},{16,17},{25,24},{24,25},{3,2},{2,3... | collective-permute-start | bytes 1966088 | tf_op jit(solution)/shard_map/ppermute | solution.py:30
  116.2 14.2 %collective-permute-start.30 = (bf16[5,8,32,256]{3,2,1,0:T(8,128)(2,1)}, bf16[5,8,32,256]{3,2,1,0:T(8,128)(2,1)}, u32[]{:S(2)}, u32[]{:S(2)}) collective-permute-start(bf16[5,8,32,256]{3,2,1,0:T(8,128)(2,1)} %collective-permute-done.22.refs_7_), channel_id=1, source_target_pairs={{1,0},{0,1},{9,8},{8,9},{17,16},{16,17},{25,24},{24,25},{3,2},{2,3... | collective-permute-start | bytes 1966088 | tf_op jit(solution)/shard_map/ppermute | solution.py:30
  125.9 17.5 %collective-permute-start.1 = (bf16[16,64,256]{2,1,0:T(8,128)(2,1)S(1)}, bf16[16,64,256]{2,1,0:T(8,128)(2,1)S(1)}, u32[]{:S(2)}, u32[]{:S(2)}) collective-permute-start(bf16[16,64,256]{2,1,0:T(8,128)(2,1)S(1)} %bitcast.27), channel_id=1, source_target_pairs={{128,0},{129,1},{136,8},{137,9},{144,16},{145,17},{152,24},{153,25... | collective-permute-start | bytes 1572872 | tf_op jit(solution)/shard_map/ppermute | solution.py:30
  126.9 26.2 %collective-permute-start.2 = (bf16[16,64,256]{2,1,0:T(8,128)(2,1)S(1)}, bf16[16,64,256]{2,1,0:T(8,128)(2,1)S(1)}, u32[]{:S(2)}, u32[]{:S(2)}) collective-permute-start(bf16[16,64,256]{2,1,0:T(8,128)(2,1)S(1)} %bitcast.28), channel_id=1, source_target_pairs={{192,0},{193,1},{200,8},{201,9},{208,16},{209,17},{216,24},{217,25... | collective-permute-start | bytes 1572872 | tf_op jit(solution)/shard_map/ppermute | solution.py:30
  126.9 26.2 %collective-permute-start.4 = (bf16[16,64,256]{2,1,0:T(8,128)(2,1)S(1)}, bf16[16,64,256]{2,1,0:T(8,128)(2,1)S(1)}, u32[]{:S(2)}, u32[]{:S(2)}) collective-permute-start(bf16[16,64,256]{2,1,0:T(8,128)(2,1)S(1)} %collective-permute-done.3.refs_4_), channel_id=1, source_target_pairs={{64,0},{65,1},{72,8},{73,9},{80,16},{81,17},{88,24},{89,25},{66,2}... | collective-permute-start | bytes 1572872 | tf_op jit(solution)/shard_map/ppermute | solution.py:30
  129.5 33.9 %collective-permute-start.5 = (bf16[16,64,256]{2,1,0:T(8,128)(2,1)S(1)}, bf16[16,64,256]{2,1,0:T(8,128)(2,1)S(1)}, u32[]{:S(2)}, u32[]{:S(2)}) collective-permute-start(bf16[16,64,256]{2,1,0:T(8,128)(2,1)S(1)} %collective-permute-done.3.refs_4_), channel_id=1, source_target_pairs={{128,0},{129,1},{136,8},{137,9},{144,16},{145,17},{152,24},{153,25... | collective-permute-start | bytes 1572872 | tf_op jit(solution)/shard_map/ppermute | solution.py:30
  130.5 44.6 %collective-permute-start.6 = (bf16[16,64,256]{2,1,0:T(8,128)(2,1)S(1)}, bf16[16,64,256]{2,1,0:T(8,128)(2,1)S(1)}, u32[]{:S(2)}, u32[]{:S(2)}) collective-permute-start(bf16[16,64,256]{2,1,0:T(8,128)(2,1)S(1)} %collective-permute-done.3.refs_4_), channel_id=1, source_target_pairs={{192,0},{193,1},{200,8},{201,9},{208,16},{209,17},{216,24},{217,25... | collective-permute-start | bytes 1572872 | tf_op jit(solution)/shard_map/ppermute | solution.py:30
  (13 other events, 141.9 us)

commit v2 on v1

v2 whole, which is shorter than its diff:
```python
import jax
import jax.numpy as jnp
from jax import lax
from jax.experimental import pallas as pl
from jax.experimental.pallas import tpu as pltpu
from jax.sharding import PartitionSpec as P

X, ZH, Y, ZL, CORE = 4, 2, 4, 4, 2
Z = ZH * ZL
COLS = Y * ZL * CORE
PARTIAL = jnp.bfloat16
GROUPS = ((0,), (1, 7), (2, 6), (3, 5, 4))


def linear(x, zh, y, zl, core):
    return (((x % X * ZH + zh % ZH) * Y + y % Y) * ZL + zl % ZL) * CORE + core % CORE


def fetch(array, dx=0, dy=0, dz=0, dcore=0):
    perm = []
    for x in range(X):
        for z in range(Z):
            for y in range(Y):
                for core in range(CORE):
                    far = (z + dz) % Z
                    perm.append((
                        linear(x + dx, far // ZL, y + dy, far % ZL, core + dcore),
                        linear(x, z // ZL, y, z % ZL, core),
                    ))
    return lax.ppermute(array, ("row", "col"), perm)


def place():
    row, col = lax.axis_index("row"), lax.axis_index("col")
    return lax.rem(row, ZH), col // (ZL * CORE), lax.rem(col // CORE, ZL), lax.rem(col, CORE)


def integrals_kernel(*refs):
    pieces, (own_ref, other_ref, own_out, other_out) = refs[:-4], refs[-4:]
    zh, _, zl, _ = place()
    swapped = [lax.rem((zh * ZL + zl + step) // ZL, ZH) != 0 for step in range(ZL)]
    rows = []
    for dy in range(Y):
        held = {}
        for g, group in enumerate(GROUPS):
            for i, dz in enumerate(group):
                held[dz] = pieces[dy * len(GROUPS) + g][i, 0]
        for step in range(ZL):
            near, far = held[step], held[step + ZL]
            low = jnp.where(swapped[step], far, near)
            high = jnp.where(swapped[step], near, far)
            rows.append(jnp.concatenate([low, high], axis=1))
    window = jnp.concatenate(rows, axis=0)
    for vectors_ref, out_ref in ((own_ref, own_out), (other_ref, other_out)):
        block = jnp.dot(vectors_ref[...], window, preferred_element_type=jnp.float32)
        out_ref[...] = block.astype(out_ref.dtype)


def integrals_of(pieces, own, other):
    _, n_a, q_part, c_part = pieces[0].shape
    rows, n_q = own.shape
    n_c = c_part * ZH
    specs = [
        pl.BlockSpec((piece.shape[0], 1, q_part, c_part), lambda a: (0, a, 0, 0)) for piece in pieces
    ]
    out = jax.ShapeDtypeStruct((rows, n_a * n_c), jnp.bfloat16)
    return pl.pallas_call(
        integrals_kernel,
        grid=(n_a,),
        out_shape=(out, out),
        in_specs=specs + [pl.BlockSpec((rows, n_q), lambda a: (0, 0))] * 2,
        out_specs=(pl.BlockSpec((rows, n_c), lambda a: (0, a)),) * 2,
        compiler_params=pltpu.CompilerParams(vmem_limit_bytes=24 << 20),
        cost_estimate=pl.CostEstimate(
            flops=4 * rows * n_q * n_a * n_c, transcendentals=0,
            bytes_accessed=2 * (n_q * n_a * n_c + 2 * rows * n_q + 2 * rows * n_a * n_c),
        ),
    )(*pieces, own, other)


def ladder_kernel(*refs, n_a, n_b, n_c, d_block):
    amps, sums, (out_ref, acc_ref) = refs[:-4], refs[-4:-2], refs[-2:]
    zh = place()[0]
    block = pl.program_id(0)

    @pl.when(block == 0)
    def _():
        acc_ref[...] = jnp.zeros_like(acc_ref)

    total = acc_ref[...]
    for half, integrals_ref in enumerate(sums):
        held = amps[half * ZH * X:(half + 1) * ZH * X]
        for d in range(d_block):
            near = jnp.concatenate([held[i][d] for i in range(X)], axis=0)
            far = jnp.concatenate([held[X + i][d] for i in range(X)], axis=0)
            low, high = jnp.where(zh != 0, far, near), jnp.where(zh != 0, near, far)
            amplitudes = jnp.concatenate([low, high], axis=0)
            stacked = jnp.concatenate(
                [integrals_ref[d * n_b:(d + 1) * n_b, a * n_c:(a + 1) * n_c] for a in range(n_a)], axis=0)
            total += jnp.dot(stacked, amplitudes, preferred_element_type=jnp.float32)
    acc_ref[...] = total

    @pl.when(block == pl.num_programs(0) - 1)
    def _():
        out_ref[...] = acc_ref[...].T.astype(out_ref.dtype)


def ladder_of(integrals, amps, n_a, d_block=4):
    near, far = amps
    n_d, c_part, n_n = far[0][0].shape
    steps = n_d // d_block
    n_c = c_part * X * ZH
    n_b = integrals[0].shape[0] // n_d

    def kernel(*refs):
        ladder_kernel(*refs, n_a=n_a, n_b=n_b, n_c=n_c, d_block=d_block)

    return pl.pallas_call(
        kernel,
        grid=(steps,),
        out_shape=jax.ShapeDtypeStruct((n_n, n_a * n_b), PARTIAL),
        in_specs=[pl.BlockSpec((d_block, c_part, n_n), lambda d: (d, 0, 0))] * (2 * X)
        + [pl.BlockSpec((d_block, c_part, n_n), lambda d: (d + steps, 0, 0))] * X
        + [pl.BlockSpec((d_block, c_part, n_n), lambda d: (d, 0, 0))] * X
        + [pl.BlockSpec((d_block * n_b, n_a * n_c), lambda d: (d, 0))] * 2,
        out_specs=pl.BlockSpec((n_n, n_a * n_b), lambda d: (0, 0)),
        scratch_shapes=[pltpu.VMEM((n_a * n_b, n_n), jnp.float32)],
        compiler_params=pltpu.CompilerParams(vmem_limit_bytes=24 << 20),
        cost_estimate=pl.CostEstimate(
            flops=4 * n_d * n_b * n_a * n_c * n_n, transcendentals=0,
            bytes_accessed=4 * (n_d * n_c * n_n + n_d * n_b * n_a * n_c),
        ),
    )(*near, *far[0], *near, *far[1], *integrals)


def ordered_vectors(pair_vectors):
    n_b, n_d, n_q = pair_vectors.shape
    _, y, zl, _ = place()
    part = n_q // (Y * ZL)
    position = jnp.arange(n_q)
    far, q = position // part, position % part
    source = ((y + far // ZL) % Y * ZL + (zl + far % ZL) % ZL) * part + q
    picked = (jnp.arange(n_q)[:, None] == source[None, :]).astype(pair_vectors.dtype)
    moved = pair_vectors.transpose(1, 0, 2).reshape(n_d * n_b, n_q)
    own = jnp.dot(moved, picked, preferred_element_type=jnp.float32).astype(pair_vectors.dtype)
    return own, fetch(own, dcore=1)


def kept_and_given(array, axis):
    low, high = jnp.split(array, 2, axis=axis)
    first = place()[3] == 0
    return jnp.where(first, low, high), jnp.where(first, high, low)


def gathered_window(window):
    mine = window.transpose(1, 2, 0)
    half = mine.shape[2] // 2
    near = [mine] + [fetch(mine, dx=dx) for dx in range(1, X)]
    parts = jnp.concatenate([m[..., :half] for m in near] + [m[..., half:] for m in near], axis=2)
    kept, given = kept_and_given(parts, 2)
    taken = fetch(given, dcore=1)
    first = place()[3] == 0
    parts = jnp.concatenate([jnp.where(first, kept, taken), jnp.where(first, taken, kept)], axis=1)
    along_z = {0: parts}
    for dz, source, step in ((1, 0, 1), (7, 0, 7), (2, 0, 2), (6, 0, 6), (3, 2, 1), (5, 6, 7), (4, 2, 2)):
        along_z[dz] = fetch(along_z[source], dz=step)
    pieces = []
    for g, group in enumerate(GROUPS):
        block = jnp.stack([along_z[dz] for dz in group])
        up, down = fetch(block, dy=1), fetch(block, dy=3)
        source, step = {1: (up, 1), 2: (down, 3)}.get(g, (block, 2))
        pieces.append([block, up, fetch(source, dy=step), down])
    return [pieces[g][dy] for dy in range(Y) for g in range(len(GROUPS))]


def gathered_amplitudes(amplitudes):
    kept, given = kept_and_given(amplitudes.transpose(1, 0, 2), 1)
    taken = fetch(given, dcore=1)
    mine = jnp.concatenate([kept, taken], axis=0)
    near = [mine] + [fetch(mine, dx=dx) for dx in range(1, X)]
    far = []
    for part in (kept, taken):
        swap = fetch(part, dz=ZL)
        far.append([swap] + [fetch(swap, dx=dx) for dx in range(1, X)])
    return near, far


def local(chol_window, pair_vectors, amplitudes):
    n_b = pair_vectors.shape[0]
    n_a = chol_window.shape[1]
    n_n = amplitudes.shape[2]
    pieces = gathered_window(chol_window)
    amps = gathered_amplitudes(amplitudes)
    integrals = integrals_of(pieces, *ordered_vectors(pair_vectors))
    partial = ladder_of(integrals, amps, n_a)
    tiles = lax.all_to_all(partial.reshape(COLS, n_n // COLS, n_a * n_b), "col", 0, 0, tiled=True)
    total = jnp.sum(tiles.astype(jnp.float32), axis=0)
    return total.reshape(n_n // COLS, n_a, n_b).transpose(1, 0, 2)


def solution(mesh):
    return jax.shard_map(
        local,
        mesh=mesh,
        in_specs=(P("row", None, "col"), P("row", "col", None), P("row", "col", None)),
        out_specs=P(None, "col", "row"),
        check_vma=False,
    )
```

time: 198 us -> 158 us (0.80)
  waiting for transfers between devices: 81.8 us -> 54.3 us
  starting transfers between devices: 68.9 us -> 55.9 us
  blocking collectives: 18.8 us -> 24.2 us
  local copies, waits for them, and re-layouts: 6.87 us -> 4.87 us
    ppermute x31 -> x36, waiting for transfers between devices: 81.8 us -> 54.3 us  [fetch(): return lax.ppermute(array, ('row', 'col'), perm)]
    ppermute x31 -> x36, starting transfers between devices: 68.9 us -> 55.9 us  [fetch(): return lax.ppermute(array, ('row', 'col'), perm)]
    all_to_all x1, blocking collectives: 18.8 us -> 24.2 us  [local(): lax.all_to_all(partial.reshape(COLS, n_n // COLS, n_a * n_b), 'col', 0, 0...]
    unnamed x18 -> x4, local copies, waits for them, and re-layouts: 6.15 us -> 2.91 us
  transfers between devices with their start and end apart: 31 -> 36, of which waited for: 12 -> 15; matrix products, arithmetic and copies ran while one was open for 5% -> 4% of each run, Pallas kernels for 7% -> 8%
where the time goes in v2:
time: 158 us
  starting transfers between devices  55.9 us (35%)
  waiting for transfers between devices  54.3 us (34%)
  blocking collectives  24.2 us (15%)
  Pallas kernels  15.2 us (10%)
  local copies, waits for them, and re-layouts  4.87 us (3%)
  matrix products  2.41 us (2%)
    ppermute x36, starting transfers between devices, fetch(): return lax.ppermute(array, ('row', 'col'), perm)  55.9 us
    ppermute x36, waiting for transfers between devices, fetch(): return lax.ppermute(array, ('row', 'col'), perm)  54.3 us
    all_to_all x1, blocking collectives, local(): lax.all_to_all(partial.reshape(COLS, n_n // COLS, n_a * n_b), 'col', 0, 0...  24.2 us
    pallas_call x1, Pallas kernels, integrals_of(): pl.pallas_call(integrals_kernel, grid=(n_a,), out_shape=(out, out), in_sp...  12 us
  transfers between devices with their start and end apart: 36, of which 15 were waited for; matrix products, arithmetic and copies ran while one was open for 4% of the time, Pallas kernels for 8%

profile of v2, /device:TPU:1, one launch (start us, length us, event | category | flops | bytes accessed | tf_op | source)
XLA Modules:
  0.0 157.7 jit_solution(9419601132934807753)
XLA Ops:
  0.0 3.3 %collective-permute-start.12 = (bf16[8,32,64]{2,1,0:T(8,128)(2,1)}, bf16[8,32,64]{2,1,0:T(8,128)(2,1)S(1)}, u32[]{:S(2)}, u32[]{:S(2)}) collective-permute-start(bf16[8,32,64]{2,1,0:T(8,128)(2,1)} %bitcast.24), channel_id=1, source_target_pairs={{64,0},{65,1},{72,8},{73,9},{80,16},{81,17},{88,24},{89,25},{66,2}... | collective-permute-start | bytes 98312 | tf_op jit(solution)/shard_map/ppermute | solution.py:30
  5.5 2.7 %copy.7 = bf16[64,16,1024]{2,0,1:T(8,128)(2,1)S(1)} copy(bf16[64,16,1024]{2,1,0:T(8,128)(2,1)} %param.4) | data formatting | bytes 4194304 | tf_op args[1]
  14.1 6.1 %collective-permute-start.18 = (bf16[8,64,128]{2,1,0:T(8,128)(2,1)S(1)}, bf16[8,64,128]{2,1,0:T(8,128)(2,1)S(1)}, u32[]{:S(2)}, u32[]{:S(2)}) collective-permute-start(bf16[8,64,128]{2,1,0:T(8,128)(2,1)S(1)} %get-tuple-element.16), channel_id=1, source_target_pairs={{4,0},{5,1},{12,8},{13,9},{20,16},{21,17},{28,24},{29,25},{6,2},{7... | collective-permute-start | bytes 393224 | tf_op jit(solution)/shard_map/ppermute | solution.py:30
  20.2 3.1 %collective-permute-start.16 = (bf16[8,64,128]{2,1,0:T(8,128)(2,1)S(1)}, bf16[8,64,128]{2,1,0:T(8,128)(2,1)S(1)}, u32[]{:S(2)}, u32[]{:S(2)}) collective-permute-start(bf16[8,64,128]{2,1,0:T(8,128)(2,1)S(1)} %get-tuple-element.16), channel_id=1, source_target_pairs={{2,0},{3,1},{10,8},{11,9},{18,16},{19,17},{26,24},{27,25},{4,2},{5... | collective-permute-start | bytes 393224 | tf_op jit(solution)/shard_map/ppermute | solution.py:30
  25.3 2.7 %collective-permute-start.23 = (bf16[1,8,64,128]{3,2,1,0:T(8,128)(2,1)S(1)}, bf16[1,8,64,128]{3,2,1,0:T(8,128)(2,1)S(1)}, u32[]{:S(2)}, u32[]{:S(2)}) collective-permute-start(bf16[1,8,64,128]{3,2,1,0:T(8,128)(2,1)S(1)} %get-tuple-element.17.refs_0_), channel_id=1, source_target_pairs={{8,0},{9,1},{16,8},{17,9},{24,16},{25,17},{0,24},{1,25},{10,2},{11... | collective-permute-start | bytes 393224 | tf_op jit(solution)/shard_map/ppermute | solution.py:30
  28.0 3.4 %collective-permute-start = (bf16[16,32,256]{2,1,0:T(8,128)(2,1)S(1)}, bf16[16,32,256]{2,1,0:T(8,128)(2,1)S(1)}, u32[]{:S(2)}, u32[]{:S(2)}) collective-permute-start(bf16[16,32,256]{2,1,0:T(8,128)(2,1)S(1)} %get-tuple-element.13), channel_id=1, source_target_pairs={{1,0},{0,1},{9,8},{8,9},{17,16},{16,17},{25,24},{24,25},{3,2},{2,3... | collective-permute-start | bytes 786440 | tf_op jit(solution)/shard_map/ppermute | solution.py:30
  31.4 2.8 %collective-permute-start.4 = (bf16[16,32,256]{2,1,0:T(8,128)(2,1)S(1)}, bf16[16,32,256]{2,1,0:T(8,128)(2,1)S(1)}, u32[]{:S(2)}, u32[]{:S(2)}) collective-permute-start(bf16[16,32,256]{2,1,0:T(8,128)(2,1)S(1)} %get-tuple-element.12), channel_id=1, source_target_pairs={{32,0},{33,1},{40,8},{41,9},{48,16},{49,17},{56,24},{57,25},{34,2}... | collective-permute-start | bytes 786440 | tf_op jit(solution)/shard_map/ppermute | solution.py:30
  35.8 4.5 %collective-permute-done.27.refs_8_ = bf16[1,8,64,128]{3,2,1,0:T(8,128)(2,1)S(1)} collective-permute-done((bf16[1,8,64,128]{3,2,1,0:T(8,128)(2,1)S(1)}, bf16[1,8,64,128]{3,2,1,0:T(8,128)(2,1)S(1)}, u32[]{:S(2)}, u32[]{:S(2)}) %collective-permute-start.27) | collective-permute-done | bytes 131104 | tf_op jit(solution)/shard_map/ppermute | solution.py:30
  40.5 3.3 %collective-permute-done.32.refs_12_ = bf16[1,8,64,128]{3,2,1,0:T(8,128)(2,1)S(1)} collective-permute-done((bf16[1,8,64,128]{3,2,1,0:T(8,128)(2,1)S(1)}, bf16[1,8,64,128]{3,2,1,0:T(8,128)(2,1)S(1)}, u32[]{:S(2)}, u32[]{:S(2)}) %collective-permute-start.32) | collective-permute-done | bytes 131104 | tf_op jit(solution)/shard_map/ppermute | solution.py:30
  43.8 2.7 %collective-permute-start.25 = (bf16[2,8,64,128]{3,2,1,0:T(8,128)(2,1)S(1)}, bf16[2,8,64,128]{3,2,1,0:T(8,128)(2,1)S(1)}, u32[]{:S(2)}, u32[]{:S(2)}) collective-permute-start(bf16[2,8,64,128]{3,2,1,0:T(8,128)(2,1)S(1)} %pad_maximum_fusion.3.refs_2_), channel_id=1, source_target_pairs={{8,0},{9,1},{16,8},{17,9},{24,16},{25,17},{0,24},{1,25},{10,2},{11... | collective-permute-start | bytes 786440 | tf_op jit(solution)/shard_map/ppermute | solution.py:30
  46.5 3.2 %collective-permute-start.21 = (bf16[8,64,128]{2,1,0:T(8,128)(2,1)S(1)}, bf16[8,64,128]{2,1,0:T(8,128)(2,1)S(1)}, u32[]{:S(2)}, u32[]{:S(2)}) collective-permute-start(bf16[8,64,128]{2,1,0:T(8,128)(2,1)S(1)} %collective-permute-done.19), channel_id=1, source_target_pairs={{38,0},{39,1},{46,8},{47,9},{54,16},{55,17},{62,24},{63,25},{0,2},... | collective-permute-start | bytes 393224 | tf_op jit(solution)/shard_map/ppermute | solution.py:30
  49.6 2.4 %collective-permute-start.22 = (bf16[8,64,128]{2,1,0:T(8,128)(2,1)S(1)}, bf16[8,64,128]{2,1,0:T(8,128)(2,1)S(1)}, u32[]{:S(2)}, u32[]{:S(2)}) collective-permute-start(bf16[8,64,128]{2,1,0:T(8,128)(2,1)S(1)} %collective-permute-done.18), channel_id=1, source_target_pairs={{4,0},{5,1},{12,8},{13,9},{20,16},{21,17},{28,24},{29,25},{6,2},{7... | collective-permute-start | bytes 393224 | tf_op jit(solution)/shard_map/ppermute | solution.py:30
  52.1 4.5 %collective-permute-start.24 = (bf16[2,8,64,128]{3,2,1,0:T(8,128)(2,1)S(1)}, bf16[2,8,64,128]{3,2,1,0:T(8,128)(2,1)S(1)}, u32[]{:S(2)}, u32[]{:S(2)}) collective-permute-start(bf16[2,8,64,128]{3,2,1,0:T(8,128)(2,1)S(1)} %pad_maximum_fusion.2.refs_1_), channel_id=1, source_target_pairs={{8,0},{9,1},{16,8},{17,9},{24,16},{25,17},{0,24},{1,25},{10,2},{11... | collective-permute-start | bytes 786440 | tf_op jit(solution)/shard_map/ppermute | solution.py:30
  61.2 5.0 %collective-permute-done.33.refs_13_ = bf16[2,8,64,128]{3,2,1,0:T(8,128)(2,1)S(1)} collective-permute-done((bf16[2,8,64,128]{3,2,1,0:T(8,128)(2,1)S(1)}, bf16[2,8,64,128]{3,2,1,0:T(8,128)(2,1)S(1)}, u32[]{:S(2)}, u32[]{:S(2)}) %collective-permute-start.33) | collective-permute-done | bytes 262176 | tf_op jit(solution)/shard_map/ppermute | solution.py:30
  66.8 4.6 %collective-permute-done.8.refs_12_ = bf16[16,32,256]{2,1,0:T(8,128)(2,1)S(1)} collective-permute-done((bf16[16,32,256]{2,1,0:T(8,128)(2,1)S(1)}, bf16[16,32,256]{2,1,0:T(8,128)(2,1)S(1)}, u32[]{:S(2)}, u32[]{:S(2)}) %collective-permute-start.8) | collective-permute-done | bytes 262176 | tf_op jit(solution)/shard_map/ppermute | solution.py:30
  76.2 5.1 %collective-permute-done.26.refs_7_ = bf16[3,8,64,128]{3,2,1,0:T(8,128)(2,1)S(1)} collective-permute-done((bf16[3,8,64,128]{3,2,1,0:T(8,128)(2,1)S(1)}, bf16[3,8,64,128]{3,2,1,0:T(8,128)(2,1)S(1)}, u32[]{:S(2)}, u32[]{:S(2)}) %collective-permute-start.26) | collective-permute-done | bytes 393248 | tf_op jit(solution)/shard_map/ppermute | solution.py:30
  82.0 5.5 %collective-permute-start.28 = (bf16[2,8,64,128]{3,2,1,0:T(8,128)(2,1)S(1)}, bf16[2,8,64,128]{3,2,1,0:T(8,128)(2,1)S(1)}, u32[]{:S(2)}, u32[]{:S(2)}) collective-permute-start(bf16[2,8,64,128]{3,2,1,0:T(8,128)(2,1)S(1)} %collective-permute-done.24.refs_5_), channel_id=1, source_target_pairs={{8,0},{9,1},{16,8},{17,9},{24,16},{25,17},{0,24},{1,25},{10,2},{11... | collective-permute-start | bytes 786440 | tf_op jit(solution)/shard_map/ppermute | solution.py:30
  87.6 5.2 %collective-permute-done.34.refs_15_ = bf16[3,8,64,128]{3,2,1,0:T(8,128)(2,1)S(1)} collective-permute-done((bf16[3,8,64,128]{3,2,1,0:T(8,128)(2,1)S(1)}, bf16[3,8,64,128]{3,2,1,0:T(8,128)(2,1)S(1)}, u32[]{:S(2)}, u32[]{:S(2)}) %collective-permute-start.34) | collective-permute-done | bytes 393248 | tf_op jit(solution)/shard_map/ppermute | solution.py:30
  94.2 4.1 %collective-permute-done.30.refs_10_ = bf16[2,8,64,128]{3,2,1,0:T(8,128)(2,1)S(1)} collective-permute-done((bf16[2,8,64,128]{3,2,1,0:T(8,128)(2,1)S(1)}, bf16[2,8,64,128]{3,2,1,0:T(8,128)(2,1)S(1)}, u32[]{:S(2)}, u32[]{:S(2)}) %collective-permute-start.30) | collective-permute-done | bytes 262176 | tf_op jit(solution)/shard_map/ppermute | solution.py:30
  102.6 12.0 %shard_map.37 = (bf16[1024,2048]{1,0:T(8,128)(2,1)S(1)}, bf16[1024,2048]{1,0:T(8,128)(2,1)S(1)}) custom-call(bf16[1,8,64,128]{3,2,1,0:T(8,128)(2,1)S(1)} %get-tuple-element.17.refs_0_, bf16[2,8,64,128]{3,2,1,0:T(8,128)(2,1)S(1)} %pad_maximum_fusion.2.refs_1_, bf16[2,8,64,128]{3,2,1,0:T(8,128)(2,1)S(1)} %pad_maximum_fusion.3.refs_2_, ...), custom_call_target="tpu_custom_call" | custom-call | flops 8589934592 | bytes 16777216 | tf_op jit(solution)/shard_map/pallas_call | solution.py:67
  114.6 6.5 %collective-permute-done.3.refs_3_.refs_11_ = bf16[32,32,256]{2,1,0:T(8,128)(2,1)S(1)} collective-permute-done((bf16[32,32,256]{2,1,0:T(8,128)(2,1)S(1)}, bf16[32,32,256]{2,1,0:T(8,128)(2,1)S(1)}, u32[]{:S(2)}, u32[]{:S(2)}) %collective-permute-start.3) | collective-permute-done | bytes 524320 | tf_op jit(solution)/shard_map/ppermute | solution.py:30
  121.1 8.4 %collective-permute-done.11.refs_15_ = bf16[16,32,256]{2,1,0:T(8,128)(2,1)S(1)} collective-permute-done((bf16[16,32,256]{2,1,0:T(8,128)(2,1)S(1)}, bf16[16,32,256]{2,1,0:T(8,128)(2,1)S(1)}, u32[]{:S(2)}, u32[]{:S(2)}) %collective-permute-start.11) | collective-permute-done | bytes 262176 | tf_op jit(solution)/shard_map/ppermute | solution.py:30
  129.5 3.2 %shard_map.38 = bf16[256,512]{1,0:T(8,128)(2,1)S(1)} custom-call(bf16[32,32,256]{2,1,0:T(8,128)(2,1)S(1)} %pad_maximum_fusion.refs_0_.refs_8_, bf16[32,32,256]{2,1,0:T(8,128)(2,1)S(1)} %collective-permute-done.1.refs_1_.refs_9_, bf16[32,32,256]{2,1,0:T(8,128)(2,1)S(1)} %collective-permute-done.2.refs_2_.refs_10_, ...), custom_call_target="tpu_custom_call" | custom-call | flops 2147483648 | bytes 12582912 | tf_op jit(solution)/shard_map/pallas_call | solution.py:118
  132.7 24.2 %all_to_all.5 = bf16[32,8,512]{2,1,0:T(8,128)(2,1)S(1)} all-to-all(bf16[32,8,512]{2,1,0:T(8,128)(2,1)S(1)} %bitcast.21), channel_id=1, replica_groups=mesh['row'=8,'col'=32] {'col'}, dimensions={0} | all-to-all | bytes 524288 | tf_op jit(solution)/shard_map/all_to_all | solution.py:196
  (72 shorter events, 28.8 us)
Async XLA Ops:
  13.7 87.9 %collective-permute-start.35 = (bf16[1024,1024]{1,0:T(8,128)(2,1)S(1)}, bf16[1024,1024]{1,0:T(8,128)(2,1)S(1)}, u32[]{:S(2)}, u32[]{:S(2)}) collective-permute-start(bf16[1024,1024]{1,0:T(8,128)(2,1)S(1)} %convert_bitcast_fusion.refs_16_), channel_id=1, source_target_pairs={{1,0},{0,1},{9,8},{8,9},{17,16},{16,17},{25,24},{24,25},{3,2},{2,3... | collective-permute-start | bytes 6291464 | tf_op jit(solution)/shard_map/ppermute | solution.py:30
  14.1 11.2 %collective-permute-start.18 = (bf16[8,64,128]{2,1,0:T(8,128)(2,1)S(1)}, bf16[8,64,128]{2,1,0:T(8,128)(2,1)S(1)}, u32[]{:S(2)}, u32[]{:S(2)}) collective-permute-start(bf16[8,64,128]{2,1,0:T(8,128)(2,1)S(1)} %get-tuple-element.16), channel_id=1, source_target_pairs={{4,0},{5,1},{12,8},{13,9},{20,16},{21,17},{28,24},{29,25},{6,2},{7... | collective-permute-start | bytes 393224 | tf_op jit(solution)/shard_map/ppermute | solution.py:30
  20.2 11.3 %collective-permute-start.16 = (bf16[8,64,128]{2,1,0:T(8,128)(2,1)S(1)}, bf16[8,64,128]{2,1,0:T(8,128)(2,1)S(1)}, u32[]{:S(2)}, u32[]{:S(2)}) collective-permute-start(bf16[8,64,128]{2,1,0:T(8,128)(2,1)S(1)} %get-tuple-element.16), channel_id=1, source_target_pairs={{2,0},{3,1},{10,8},{11,9},{18,16},{19,17},{26,24},{27,25},{4,2},{5... | collective-permute-start | bytes 393224 | tf_op jit(solution)/shard_map/ppermute | solution.py:30
  23.3 11.0 %collective-permute-start.17 = (bf16[8,64,128]{2,1,0:T(8,128)(2,1)S(1)}, bf16[8,64,128]{2,1,0:T(8,128)(2,1)S(1)}, u32[]{:S(2)}, u32[]{:S(2)}) collective-permute-start(bf16[8,64,128]{2,1,0:T(8,128)(2,1)S(1)} %get-tuple-element.16), channel_id=1, source_target_pairs={{38,0},{39,1},{46,8},{47,9},{54,16},{55,17},{62,24},{63,25},{0,2},... | collective-permute-start | bytes 393224 | tf_op jit(solution)/shard_map/ppermute | solution.py:30
  25.3 10.1 %collective-permute-start.23 = (bf16[1,8,64,128]{3,2,1,0:T(8,128)(2,1)S(1)}, bf16[1,8,64,128]{3,2,1,0:T(8,128)(2,1)S(1)}, u32[]{:S(2)}, u32[]{:S(2)}) collective-permute-start(bf16[1,8,64,128]{3,2,1,0:T(8,128)(2,1)S(1)} %get-tuple-element.17.refs_0_), channel_id=1, source_target_pairs={{8,0},{9,1},{16,8},{17,9},{24,16},{25,17},{0,24},{1,25},{10,2},{11... | collective-permute-start | bytes 393224 | tf_op jit(solution)/shard_map/ppermute | solution.py:30
  28.0 15.8 %collective-permute-start = (bf16[16,32,256]{2,1,0:T(8,128)(2,1)S(1)}, bf16[16,32,256]{2,1,0:T(8,128)(2,1)S(1)}, u32[]{:S(2)}, u32[]{:S(2)}) collective-permute-start(bf16[16,32,256]{2,1,0:T(8,128)(2,1)S(1)} %get-tuple-element.13), channel_id=1, source_target_pairs={{1,0},{0,1},{9,8},{8,9},{17,16},{16,17},{25,24},{24,25},{3,2},{2,3... | collective-permute-start | bytes 786440 | tf_op jit(solution)/shard_map/ppermute | solution.py:30
  31.4 15.0 %collective-permute-start.4 = (bf16[16,32,256]{2,1,0:T(8,128)(2,1)S(1)}, bf16[16,32,256]{2,1,0:T(8,128)(2,1)S(1)}, u32[]{:S(2)}, u32[]{:S(2)}) collective-permute-start(bf16[16,32,256]{2,1,0:T(8,128)(2,1)S(1)} %get-tuple-element.12), channel_id=1, source_target_pairs={{32,0},{33,1},{40,8},{41,9},{48,16},{49,17},{56,24},{57,25},{34,2}... | collective-permute-start | bytes 786440 | tf_op jit(solution)/shard_map/ppermute | solution.py:30
  40.3 9.4 %collective-permute-start.20 = (bf16[8,64,128]{2,1,0:T(8,128)(2,1)S(1)}, bf16[8,64,128]{2,1,0:T(8,128)(2,1)S(1)}, u32[]{:S(2)}, u32[]{:S(2)}) collective-permute-start(bf16[8,64,128]{2,1,0:T(8,128)(2,1)S(1)} %collective-permute-done.18), channel_id=1, source_target_pairs={{2,0},{3,1},{10,8},{11,9},{18,16},{19,17},{26,24},{27,25},{4,2},{5... | collective-permute-start | bytes 393224 | tf_op jit(solution)/shard_map/ppermute | solution.py:30
  43.8 14.5 %collective-permute-start.29 = (bf16[2,8,64,128]{3,2,1,0:T(8,128)(2,1)S(1)}, bf16[2,8,64,128]{3,2,1,0:T(8,128)(2,1)S(1)}, u32[]{:S(2)}, u32[]{:S(2)}) collective-permute-start(bf16[2,8,64,128]{3,2,1,0:T(8,128)(2,1)S(1)} %pad_maximum_fusion.3.refs_2_), channel_id=1, source_target_pairs={{24,0},{25,1},{0,8},{1,9},{8,16},{9,17},{16,24},{17,25},{26,2},{27... | collective-permute-start | bytes 786440 | tf_op jit(solution)/shard_map/ppermute | solution.py:30
  43.8 14.5 %collective-permute-start.25 = (bf16[2,8,64,128]{3,2,1,0:T(8,128)(2,1)S(1)}, bf16[2,8,64,128]{3,2,1,0:T(8,128)(2,1)S(1)}, u32[]{:S(2)}, u32[]{:S(2)}) collective-permute-start(bf16[2,8,64,128]{3,2,1,0:T(8,128)(2,1)S(1)} %pad_maximum_fusion.3.refs_2_), channel_id=1, source_target_pairs={{8,0},{9,1},{16,8},{17,9},{24,16},{25,17},{0,24},{1,25},{10,2},{11... | collective-permute-start | bytes 786440 | tf_op jit(solution)/shard_map/ppermute | solution.py:30
  58.3 13.1 %collective-permute-start.8 = (bf16[16,32,256]{2,1,0:T(8,128)(2,1)S(1)}, bf16[16,32,256]{2,1,0:T(8,128)(2,1)S(1)}, u32[]{:S(2)}, u32[]{:S(2)}) collective-permute-start(bf16[16,32,256]{2,1,0:T(8,128)(2,1)S(1)} %collective-permute-done), channel_id=1, source_target_pairs={{32,0},{33,1},{40,8},{41,9},{48,16},{49,17},{56,24},{57,25},{34,2}... | collective-permute-start | bytes 786440 | tf_op jit(solution)/shard_map/ppermute | solution.py:30
  58.3 15.5 %collective-permute-start.5 = (bf16[16,32,256]{2,1,0:T(8,128)(2,1)S(1)}, bf16[16,32,256]{2,1,0:T(8,128)(2,1)S(1)}, u32[]{:S(2)}, u32[]{:S(2)}) collective-permute-start(bf16[16,32,256]{2,1,0:T(8,128)(2,1)S(1)} %collective-permute-done.4.refs_4_), channel_id=1, source_target_pairs={{64,0},{65,1},{72,8},{73,9},{80,16},{81,17},{88,24},{89,25},{66,2}... | collective-permute-start | bytes 786440 | tf_op jit(solution)/shard_map/ppermute | solution.py:30
  60.1 13.7 %collective-permute-start.6 = (bf16[16,32,256]{2,1,0:T(8,128)(2,1)S(1)}, bf16[16,32,256]{2,1,0:T(8,128)(2,1)S(1)}, u32[]{:S(2)}, u32[]{:S(2)}) collective-permute-start(bf16[16,32,256]{2,1,0:T(8,128)(2,1)S(1)} %collective-permute-done.4.refs_4_), channel_id=1, source_target_pairs={{128,0},{129,1},{136,8},{137,9},{144,16},{145,17},{152,24},{153,25... | collective-permute-start | bytes 786440 | tf_op jit(solution)/shard_map/ppermute | solution.py:30
  66.2 9.9 %collective-permute-start.7 = (bf16[16,32,256]{2,1,0:T(8,128)(2,1)S(1)}, bf16[16,32,256]{2,1,0:T(8,128)(2,1)S(1)}, u32[]{:S(2)}, u32[]{:S(2)}) collective-permute-start(bf16[16,32,256]{2,1,0:T(8,128)(2,1)S(1)} %collective-permute-done.4.refs_4_), channel_id=1, source_target_pairs={{192,0},{193,1},{200,8},{201,9},{208,16},{209,17},{216,24},{217,25... | collective-permute-start | bytes 786440 | tf_op jit(solution)/shard_map/ppermute | solution.py:30
  71.4 9.9 %collective-permute-start.26 = (bf16[3,8,64,128]{3,2,1,0:T(8,128)(2,1)S(1)}, bf16[3,8,64,128]{3,2,1,0:T(8,128)(2,1)S(1)}, u32[]{:S(2)}, u32[]{:S(2)}) collective-permute-start(bf16[3,8,64,128]{3,2,1,0:T(8,128)(2,1)S(1)} %pad_maximum_fusion.1.refs_3_), channel_id=1, source_target_pairs={{8,0},{9,1},{16,8},{17,9},{24,16},{25,17},{0,24},{1,25},{10,2},{11... | collective-permute-start | bytes 1179656 | tf_op jit(solution)/shard_map/ppermute | solution.py:30
  73.9 26.0 %collective-permute-start.1 = (bf16[32,32,256]{2,1,0:T(8,128)(2,1)S(1)}, bf16[32,32,256]{2,1,0:T(8,128)(2,1)S(1)}, u32[]{:S(2)}, u32[]{:S(2)}) collective-permute-start(bf16[32,32,256]{2,1,0:T(8,128)(2,1)S(1)} %pad_maximum_fusion.refs_0_.refs_8_), channel_id=1, source_target_pairs={{64,0},{65,1},{72,8},{73,9},{80,16},{81,17},{88,24},{89,25},{66,2}... | collective-permute-start | bytes 1572872 | tf_op jit(solution)/shard_map/ppermute | solution.py:30
  76.1 16.6 %collective-permute-start.34 = (bf16[3,8,64,128]{3,2,1,0:T(8,128)(2,1)S(1)}, bf16[3,8,64,128]{3,2,1,0:T(8,128)(2,1)S(1)}, u32[]{:S(2)}, u32[]{:S(2)}) collective-permute-start(bf16[3,8,64,128]{3,2,1,0:T(8,128)(2,1)S(1)} %pad_maximum_fusion.1.refs_3_), channel_id=1, source_target_pairs={{24,0},{25,1},{0,8},{1,9},{8,16},{9,17},{16,24},{17,25},{26,2},{27... | collective-permute-start | bytes 1179656 | tf_op jit(solution)/shard_map/ppermute | solution.py:30
  81.3 17.0 %collective-permute-start.30 = (bf16[2,8,64,128]{3,2,1,0:T(8,128)(2,1)S(1)}, bf16[2,8,64,128]{3,2,1,0:T(8,128)(2,1)S(1)}, u32[]{:S(2)}, u32[]{:S(2)}) collective-permute-start(bf16[2,8,64,128]{3,2,1,0:T(8,128)(2,1)S(1)} %collective-permute-done.29.refs_14_), channel_id=1, source_target_pairs={{24,0},{25,1},{0,8},{1,9},{8,16},{9,17},{16,24},{17,25},{26,2},{27... | collective-permute-start | bytes 786440 | tf_op jit(solution)/shard_map/ppermute | solution.py:30
  82.0 16.5 %collective-permute-start.28 = (bf16[2,8,64,128]{3,2,1,0:T(8,128)(2,1)S(1)}, bf16[2,8,64,128]{3,2,1,0:T(8,128)(2,1)S(1)}, u32[]{:S(2)}, u32[]{:S(2)}) collective-permute-start(bf16[2,8,64,128]{3,2,1,0:T(8,128)(2,1)S(1)} %collective-permute-done.24.refs_5_), channel_id=1, source_target_pairs={{8,0},{9,1},{16,8},{17,9},{24,16},{25,17},{0,24},{1,25},{10,2},{11... | collective-permute-start | bytes 786440 | tf_op jit(solution)/shard_map/ppermute | solution.py:30
  92.7 21.8 %collective-permute-start.2 = (bf16[32,32,256]{2,1,0:T(8,128)(2,1)S(1)}, bf16[32,32,256]{2,1,0:T(8,128)(2,1)S(1)}, u32[]{:S(2)}, u32[]{:S(2)}) collective-permute-start(bf16[32,32,256]{2,1,0:T(8,128)(2,1)S(1)} %pad_maximum_fusion.refs_0_.refs_8_), channel_id=1, source_target_pairs={{128,0},{129,1},{136,8},{137,9},{144,16},{145,17},{152,24},{153,25... | collective-permute-start | bytes 1572872 | tf_op jit(solution)/shard_map/ppermute | solution.py:30
  98.3 22.8 %collective-permute-start.3 = (bf16[32,32,256]{2,1,0:T(8,128)(2,1)S(1)}, bf16[32,32,256]{2,1,0:T(8,128)(2,1)S(1)}, u32[]{:S(2)}, u32[]{:S(2)}) collective-permute-start(bf16[32,32,256]{2,1,0:T(8,128)(2,1)S(1)} %pad_maximum_fusion.refs_0_.refs_8_), channel_id=1, source_target_pairs={{192,0},{193,1},{200,8},{201,9},{208,16},{209,17},{216,24},{217,25... | collective-permute-start | bytes 1572872 | tf_op jit(solution)/shard_map/ppermute | solution.py:30
  98.6 22.5 %collective-permute-start.10 = (bf16[16,32,256]{2,1,0:T(8,128)(2,1)S(1)}, bf16[16,32,256]{2,1,0:T(8,128)(2,1)S(1)}, u32[]{:S(2)}, u32[]{:S(2)}) collective-permute-start(bf16[16,32,256]{2,1,0:T(8,128)(2,1)S(1)} %collective-permute-done.8.refs_12_), channel_id=1, source_target_pairs={{128,0},{129,1},{136,8},{137,9},{144,16},{145,17},{152,24},{153,25... | collective-permute-start | bytes 786440 | tf_op jit(solution)/shard_map/ppermute | solution.py:30
  99.9 29.7 %collective-permute-start.11 = (bf16[16,32,256]{2,1,0:T(8,128)(2,1)S(1)}, bf16[16,32,256]{2,1,0:T(8,128)(2,1)S(1)}, u32[]{:S(2)}, u32[]{:S(2)}) collective-permute-start(bf16[16,32,256]{2,1,0:T(8,128)(2,1)S(1)} %collective-permute-done.8.refs_12_), channel_id=1, source_target_pairs={{192,0},{193,1},{200,8},{201,9},{208,16},{209,17},{216,24},{217,25... | collective-permute-start | bytes 786440 | tf_op jit(solution)/shard_map/ppermute | solution.py:30
  101.6 27.9 %collective-permute-start.9 = (bf16[16,32,256]{2,1,0:T(8,128)(2,1)S(1)}, bf16[16,32,256]{2,1,0:T(8,128)(2,1)S(1)}, u32[]{:S(2)}, u32[]{:S(2)}) collective-permute-start(bf16[16,32,256]{2,1,0:T(8,128)(2,1)S(1)} %collective-permute-done.8.refs_12_), channel_id=1, source_target_pairs={{64,0},{65,1},{72,8},{73,9},{80,16},{81,17},{88,24},{89,25},{66,2}... | collective-permute-start | bytes 786440 | tf_op jit(solution)/shard_map/ppermute | solution.py:30
  (13 other events, 86.4 us)
